TPU v7x, 256 devices: a whole 4x4x8 slice. The times are simulated.
256 devices in a mesh: gx: 2 (over z_lo), gy: 16 (over x, y), gz: 8 (over z_hi, core).
Axes of the slice: x: 4, y: 4, z: 8 (z_hi: 4, z_lo: 2; z = z_hi * 2 + z_lo), core: 2. Of those that a mesh axis runs over, the one named last changes fastest.
Arguments:
- factors: bfloat16 [6144, 8, 4096], P('gy', None, 'gz'), may hold values from -0.046875 to 0.046875
- trial_vectors: float32 [64, 8, 4096], P('gx', None, 'gz'), may hold values from -6 to 6
- energy_gap: float32 [8, 4096], P(None, 'gz'), may hold values from 0.5 to 4
Outputs:
- updated_vectors: float32 [64, 8, 4096], P('gx', None, 'gz')
- coupling: float32 [64, 64], P(None, 'gx')
All inputs are finite; a program needn't handle non-finite values.
Results may differ from a plain program's by a relative error of at most 0.02.
Values may be sent and summed in bfloat16 or wider, within the bound.
No kernel may reach another device: no remote copies, remote signals or barrier semaphores. Data moves between devices by JAX's collectives and lax.ppermute only.
A program may use at most 64 MiB of HBM per device.

v0:
```python
import jax
import jax.numpy as jnp
from jax import lax
from jax.sharding import PartitionSpec as P

ITERS = 2


def copy_for_each(array, axis):
    length = lax.axis_size(axis)
    return lax.all_to_all(
        jnp.broadcast_to(array[None], (length, *array.shape)), axis, 0, 0, tiled=True
    )


def over_copies(array, axis):
    everything = copy_for_each(array, axis)
    return jnp.sum(everything, axis=0)


def packed_total(arrays, axis):
    ends = [0]
    for a in arrays:
        ends.append(ends[-1] + a.size)
    so_far = over_copies(jnp.concatenate([a.ravel() for a in arrays]), axis)
    return tuple((so_far[b:e].reshape(a.shape) for a, b, e in zip(arrays, ends, ends[1:])))


def over_copies_2(array, axis):
    return copy_for_each(array, axis).astype(jnp.float32).sum(axis=0)


def padded_to(lines, length):
    spare = -lines.shape[0] % length
    if not spare:
        return lines
    return jnp.concatenate([lines, jnp.zeros((spare, *lines.shape[1:]), lines.dtype)])


def sum_in_two_steps(array, axis):
    lines = array.reshape(-1, *array.shape[1:][-1:])
    padded = padded_to(lines, lax.axis_size(axis))
    own = lax.psum_scatter(padded, axis, scatter_dimension=0, tiled=True)
    whole = lax.all_gather(own, axis, axis=0, tiled=True)
    return whole[: len(lines)].reshape(array.shape)


def in_order(tiles, dim):
    lengths = list(tiles.shape[1:])
    lengths[dim] *= tiles.shape[0]
    return jnp.moveaxis(tiles, 0, dim).reshape(lengths)


def gathered_copies(array, axis, dim):
    return in_order(copy_for_each(array, axis), dim)


def in_blocks(array, dim, length):
    lengths = array.shape
    tiles = array.reshape(*lengths[:dim], length, lengths[dim] // length, *lengths[dim + 1 :])
    return jnp.moveaxis(tiles, dim, 0)


def sum_at_owner(array, axis, dim):
    tiles = in_blocks(array, dim, lax.axis_size(axis))
    arrived = lax.all_to_all(tiles, axis, split_axis=0, concat_axis=0, tiled=True)
    return arrived.astype(jnp.float32).sum(axis=0)


def sum_by_parts(array, axes):
    lines = array.reshape(-1, array.shape[-1])
    padded = padded_to(lines, lax.axis_size(axes))
    whole = gathered_copies(sum_at_owner(padded, axes, 0).astype(jnp.bfloat16), axes, 0)
    return lax.slice_in_dim(whole, 0, len(lines)).reshape(array.shape).astype(jnp.float32)


def solve_subspace(gram_matrix, projected):
    lower_factor = jnp.linalg.cholesky(gram_matrix)
    inner_solve = lax.linalg.triangular_solve(lower_factor, projected, left_side=True, lower=True)
    return lax.linalg.triangular_solve(
        lower_factor, inner_solve, left_side=True, lower=True, transpose_a=True
    )


def correct(own_vectors, gap_share, fock_part):
    highest = lax.Precision.HIGHEST
    everyone = lax.all_gather(own_vectors.astype(jnp.bfloat16), "gx", axis=0, tiled=True).astype(
        own_vectors.dtype
    )
    sigma_own = gap_share[None, :, :] * own_vectors + fock_part
    gram_matrix = jnp.einsum("krn,lrn->kl", everyone, everyone, precision=highest)
    projected = jnp.einsum("lrn,krn->lk", everyone, sigma_own, precision=highest)
    gram_matrix, projected = packed_total((gram_matrix, projected), "gz")
    coupling = solve_subspace(gram_matrix, projected)
    residual = sigma_own - jnp.einsum("lrn,lk->krn", everyone, coupling, precision=highest)
    return (own_vectors - residual / gap_share[None, :, :], coupling)


def per_device(factors, trial_vectors, energy_gap):
    current = trial_vectors
    coupling = None
    for iteration in range(ITERS):
        compact = current.astype(jnp.bfloat16)
        fitted = jnp.einsum("prn,krn->kp", factors, compact, preferred_element_type=jnp.float32)
        fitted = over_copies_2(fitted.astype(jnp.bfloat16), "gz").astype(jnp.float32)
        mixed_fit = jnp.einsum(
            "prn,kln->klrp", factors, compact, preferred_element_type=jnp.float32
        )
        mixed_fit = (
            sum_in_two_steps(mixed_fit.astype(jnp.bfloat16), "gz")
            .astype(jnp.float32)
            .astype(jnp.bfloat16)
        )
        coulomb = jnp.einsum(
            "prn,kp->krn", factors, fitted.astype(jnp.bfloat16), preferred_element_type=jnp.float32
        )
        exchange_part = jnp.einsum(
            "klrp,pln->krn", mixed_fit, factors, preferred_element_type=jnp.float32
        )
        partial_fock = 2.0 * coulomb - exchange_part
        fock_part = sum_by_parts(partial_fock.astype(jnp.bfloat16), "gy")
        current, coupling = correct(current, energy_gap, fock_part)
    return (current, coupling)


def solution(mesh):
    placed = (P("gy", None, "gz"), P("gx", None, "gz"), P(None, "gz"))
    return jax.shard_map(
        per_device,
        mesh=mesh,
        in_specs=placed,
        out_specs=(P("gx", None, "gz"), P(None, "gx")),
        check_vma=False,
    )
```

profile of v0, /device:TPU:2, one launch (start us, length us, event | category | flops | bytes accessed | tf_op | source)
XLA Modules:
  0.0 309.3 jit_solution(6392802762433335574)
XLA Ops:
  7.2 1.3 copy.161
  8.5 4.2 %fusion.17 = bf16[32,8,8,384]{3,1,2,0:T(8,128)(2,1)S(1)} fusion(bf16[384,8,512]{2,1,0:T(8,128)(2,1)} %param.8, bf16[32,8,512,1]{2,0,1,3:T(8,128)(2,1)S(1)} %bitcast.126), kind=kOutput, calls=%fused_computation.11 | convolution fusion | flops 806092800 | bytes 4980736 | tf_op jit(solution)/shard_map/prn,kln->klrp/dot_general | solution.py:106
  12.8 1.4 copy.77
  14.3 44.3 %reduce-scatter.3.cloned.1.call-done = bf16[256,384]{1,0:T(8,128)(2,1)} async-done(((bf16[2048,384]{1,0:T(8,128)(2,1)}), bf16[256,384]{1,0:T(8,128)(2,1)}) %reduce-scatter.3.cloned.1.call-update) | async-done | bytes 196624 | tf_op jit(solution)/shard_map/reduce_scatter | solution.py:43
  58.6 1.3 copy.159
  59.9 1.8 fusion.34
  61.8 15.8 %all_to_all.42 = bf16[8,32,384]{2,1,0:T(8,128)(2,1)} all-to-all(bf16[8,32,384]{2,1,0:T(8,128)(2,1)S(1)} %broadcast_in_dim.12), channel_id=1, replica_groups=mesh['gx'=2,'gy'=16,'gz'=8] {'gz'}, dimensions={0} | all-to-all | bytes 393216 | tf_op jit(solution)/shard_map/all_to_all | solution.py:11
  78.5 13.4 %all-gather.3.cloned.1.call-done = bf16[2048,384]{1,0:T(8,128)(2,1)} async-done(((bf16[256,384]{1,0:T(8,128)(2,1)}), bf16[2048,384]{1,0:T(8,128)(2,1)}) %all-gather.3.cloned.1.call-update) | async-done | bytes 1572880 | tf_op jit(solution)/shard_map/all_gather | solution.py:44
  91.9 3.3 %fusion.20 = f32[32,8,512]{2,1,0:T(8,128)S(1)} fusion(bf16[32,8,8,384]{3,2,1,0:T(8,128)(2,1)} %bitcast.127, bf16[384,8,512]{2,1,0:T(8,128)(2,1)S(1)} %copy-done), kind=kOutput, calls=%fused_computation.12 | convolution fusion | flops 805306368 | bytes 5242880 | tf_op jit(solution)/shard_map/klrp,pln->krn/dot_general | solution.py:117
  95.2 2.1 fusion.32
  97.5 14.4 %all_to_all.43 = bf16[16,16,512]{2,1,0:T(8,128)(2,1)} all-to-all(bf16[16,16,512]{2,1,0:T(8,128)(2,1)S(1)} %bitcast.123), channel_id=1, replica_groups=mesh['gx'=2,'gy'=16,'gz'=8] {'gy'}, dimensions={0} | all-to-all | bytes 524288 | tf_op jit(solution)/shard_map/all_to_all | solution.py:66
  113.6 5.7 %all-to-all-start.2 = ((bf16[16,16,512]{2,1,0:T(8,128)(2,1)}), bf16[16,16,512]{2,1,0:T(8,128)(2,1)}, u32[]{:S(2)}, u32[]{:S(2)}) async-start(bf16[16,16,512]{2,1,0:T(8,128)(2,1)} %broadcast_in_dim.13), calls=%async_computation.3 | async-start | bytes 524288 | tf_op jit(solution)/shard_map/all_to_all | solution.py:11
  119.4 7.3 %all_gather.13 = bf16[64,8,512]{2,0,1:T(8,128)(2,1)S(1)} all-gather(bf16[32,8,512]{2,0,1:T(8,128)(2,1)S(1)} %copy.159), channel_id=1, replica_groups=mesh['gx'=2,'gy'=16,'gz'=8] {'gx'}, dimensions={0}, use_global_device_ids=true | all-gather | bytes 786432 | tf_op jit(solution)/shard_map/all_gather | solution.py:87
  129.7 2.2 convolution_bitcast_fusion.6
  132.2 13.8 %all_to_all.44 = f32[8,1,6144]{2,1,0:T(1,128)S(1)} all-to-all(f32[8,1,6144]{2,1,0:T(1,128)S(1)} %broadcast_in_dim.15), channel_id=1, replica_groups=mesh['gx'=2,'gy'=16,'gz'=8] {'gz'}, dimensions={0} | all-to-all | bytes 393216 | tf_op jit(solution)/shard_map/all_to_all | solution.py:11
  146.4 5.8 %cholesky.44 = f32[64,64]{1,0:T(8,128)S(1)} custom-call(f32[64,64]{1,0:T(8,128)S(1)} %fusion.58), custom_call_target="Cholesky" | custom-call | tf_op jit(solution)/shard_map/jit(cholesky)/cholesky | solution.py:78
  153.5 4.9 %custom-call.11 = f32[1,64,64]{1,2,0:T(8,128)S(1)} custom-call(f32[1,64,64]{2,1,0:T(8,128)S(1)} %fusion.48), custom_call_target="InvertDiagBlocksLowerTriangular" | custom-call | tf_op jit(solution)/shard_map/triangular_solve/custom-call.2 | solution.py:80
  158.9 3.1 fusion.62
  162.0 2.5 fusion.14
  164.5 1.4 copy.90
  166.0 38.9 %reduce-scatter.5.cloned.1.call-done = bf16[256,384]{1,0:T(8,128)(2,1)} async-done(((bf16[2048,384]{1,0:T(8,128)(2,1)}), bf16[256,384]{1,0:T(8,128)(2,1)}) %reduce-scatter.5.cloned.1.call-update) | async-done | bytes 196624 | tf_op jit(solution)/shard_map/reduce_scatter | solution.py:43
  204.9 1.8 fusion.35
  206.7 15.8 %all_to_all.45 = bf16[8,32,384]{2,1,0:T(8,128)(2,1)S(1)} all-to-all(bf16[8,32,384]{2,1,0:T(8,128)(2,1)S(1)} %broadcast_in_dim.16), channel_id=1, replica_groups=mesh['gx'=2,'gy'=16,'gz'=8] {'gz'}, dimensions={0} | all-to-all | bytes 393216 | tf_op jit(solution)/shard_map/all_to_all | solution.py:11
  222.6 16.8 %all-gather.5.cloned.1.call-done = bf16[2048,384]{1,0:T(8,128)(2,1)} async-done(((bf16[256,384]{1,0:T(8,128)(2,1)}), bf16[2048,384]{1,0:T(8,128)(2,1)}) %all-gather.5.cloned.1.call-update) | async-done | bytes 1572880 | tf_op jit(solution)/shard_map/all_gather | solution.py:44
  239.4 3.3 %fusion.23 = f32[32,8,512]{2,1,0:T(8,128)S(1)} fusion(bf16[32,8,8,384]{3,2,1,0:T(8,128)(2,1)} %bitcast.128, bf16[384,8,512]{2,1,0:T(8,128)(2,1)S(1)} %copy-done), kind=kOutput, calls=%fused_computation.13 | convolution fusion | flops 805306368 | bytes 5242880 | tf_op jit(solution)/shard_map/klrp,pln->krn/dot_general | solution.py:117
  242.7 2.1 fusion.33
  245.0 14.9 %all_to_all.46 = bf16[16,16,512]{2,1,0:T(8,128)(2,1)S(1)} all-to-all(bf16[16,16,512]{2,1,0:T(8,128)(2,1)S(1)} %bitcast.124), channel_id=1, replica_groups=mesh['gx'=2,'gy'=16,'gz'=8] {'gy'}, dimensions={0} | all-to-all | bytes 524288 | tf_op jit(solution)/shard_map/all_to_all | solution.py:66
  260.7 5.3 %all-to-all-start.6 = ((bf16[16,16,512]{2,1,0:T(8,128)(2,1)}), bf16[16,16,512]{2,1,0:T(8,128)(2,1)S(1)}, u32[]{:S(2)}, u32[]{:S(2)}) async-start(bf16[16,16,512]{2,1,0:T(8,128)(2,1)} %broadcast_in_dim.17), calls=%async_computation.8 | async-start | bytes 524288 | tf_op jit(solution)/shard_map/all_to_all | solution.py:11
  266.0 7.4 %all_gather.15 = bf16[64,8,512]{2,0,1:T(8,128)(2,1)S(1)} all-gather(bf16[32,8,512]{2,0,1:T(8,128)(2,1)S(1)} %copy-done.5), channel_id=1, replica_groups=mesh['gx'=2,'gy'=16,'gz'=8] {'gx'}, dimensions={0}, use_global_device_ids=true | all-gather | bytes 786432 | tf_op jit(solution)/shard_map/all_gather | solution.py:87
  275.0 13.2 %all_to_all.47 = f32[8,1,6144]{2,1,0:T(1,128)S(1)} all-to-all(f32[8,1,6144]{2,1,0:T(1,128)S(1)} %broadcast_in_dim.18), channel_id=1, replica_groups=mesh['gx'=2,'gy'=16,'gz'=8] {'gz'}, dimensions={0} | all-to-all | bytes 393216 | tf_op jit(solution)/shard_map/all_to_all | solution.py:11
  288.5 5.8 %cholesky.55 = f32[64,64]{1,0:T(8,128)S(1)} custom-call(f32[64,64]{1,0:T(8,128)S(1)} %fusion.54), custom_call_target="Cholesky" | custom-call | tf_op jit(solution)/shard_map/jit(cholesky)/cholesky | solution.py:78
  295.7 4.9 %custom-call.13 = f32[1,64,64]{1,2,0:T(8,128)S(1)} custom-call(f32[1,64,64]{2,1,0:T(8,128)S(1)} %fusion.49), custom_call_target="InvertDiagBlocksLowerTriangular" | custom-call | tf_op jit(solution)/shard_map/triangular_solve/custom-call.2 | solution.py:80
  (76 shorter events, 14.7 us)
Async XLA Ops:
  7.2 51.4 %reduce-scatter.3.cloned.1.call-start = ((), (), s32[]{:S(2)}) async-start(), calls=%async_computation.10 | async-start | bytes 1769472 | tf_op jit(solution)/shard_map/reduce_scatter | solution.py:43
  12.8 47.2 %copy-start = (bf16[384,8,512]{2,1,0:T(8,128)(2,1)S(1)}, bf16[384,8,512]{2,1,0:T(8,128)(2,1)}, u32[]{:S(2)}) copy-start(bf16[384,8,512]{2,1,0:T(8,128)(2,1)} %param.8) | copy-start | bytes 9437188
  14.3 77.6 %all-gather.3.cloned.1.call-start = ((), (), s32[]{:S(2)}) async-start(), calls=%async_computation.11 | async-start | bytes 1769472 | tf_op jit(solution)/shard_map/all_gather | solution.py:44
  97.3 32.4 %copy-start.6 = (f32[8,512]{1,0:T(8,128)S(1)}, f32[8,512]{1,0:T(8,128)}, u32[]{:S(2)}) copy-start(f32[8,512]{1,0:T(8,128)} %param.10) | copy-start | bytes 49156
  113.6 14.2 %all-to-all-start.2 = ((bf16[16,16,512]{2,1,0:T(8,128)(2,1)}), bf16[16,16,512]{2,1,0:T(8,128)(2,1)}, u32[]{:S(2)}, u32[]{:S(2)}) async-start(bf16[16,16,512]{2,1,0:T(8,128)(2,1)} %broadcast_in_dim.13), calls=%async_computation.3 | async-start | bytes 524288 | tf_op jit(solution)/shard_map/all_to_all | solution.py:11
  119.3 85.5 %reduce-scatter.5.cloned.1.call-start = ((), (), s32[]{:S(2)}) async-start(), calls=%async_computation.12 | async-start | bytes 1769472 | tf_op jit(solution)/shard_map/reduce_scatter | solution.py:43
  126.7 0.8 copy-start.1
  128.9 0.8 copy-start.2
  162.0 42.9 %copy-start.4 = (bf16[32,8,512]{2,0,1:T(8,128)(2,1)}, bf16[32,8,512]{2,0,1:T(8,128)(2,1)S(1)}, u32[]{:S(2)}) copy-start(bf16[32,8,512]{2,0,1:T(8,128)(2,1)S(1)} %get-tuple-element.13) | copy-start | bytes 786436
  165.9 73.4 %all-gather.5.cloned.1.call-start = ((), (), s32[]{:S(2)}) async-start(), calls=%async_computation.13 | async-start | bytes 1769472 | tf_op jit(solution)/shard_map/all_gather | solution.py:44
  242.7 23.3 %copy-start.5 = (bf16[32,8,512]{2,0,1:T(8,128)(2,1)S(1)}, bf16[32,8,512]{2,0,1:T(8,128)(2,1)}, u32[]{:S(2)}) copy-start(bf16[32,8,512]{2,0,1:T(8,128)(2,1)} %copy-done.4) | copy-start | bytes 786436
  244.8 29.1 %copy-start.3 = (f32[32,8,512]{2,0,1:T(8,128)S(1)}, f32[32,8,512]{2,0,1:T(8,128)}, u32[]{:S(2)}) copy-start(f32[32,8,512]{2,0,1:T(8,128)} %get-tuple-element.14) | copy-start | bytes 1572868
  260.7 13.1 %all-to-all-start.6 = ((bf16[16,16,512]{2,1,0:T(8,128)(2,1)}), bf16[16,16,512]{2,1,0:T(8,128)(2,1)S(1)}, u32[]{:S(2)}, u32[]{:S(2)}) async-start(bf16[16,16,512]{2,1,0:T(8,128)(2,1)} %broadcast_in_dim.17), calls=%async_computation.8 | async-start | bytes 524288 | tf_op jit(solution)/shard_map/all_to_all | solution.py:11
  301.1 1.7 copy-start.7
Sparse Core Ops, SparseCore 0:
  14.4 44.1 reduce-scatter.2
  60.4 31.4 all-gather.2
  166.1 38.7 reduce-scatter.4
  206.6 32.7 all-gather.4
where the time goes:
time: 310 us; the launch traced here: 309 us
  waiting for transfers between devices  113 us (36%)
  blocking collectives  103 us (33%)
  matrix products  29.2 us (9%)
  other arithmetic  27.6 us (9%)
  between operations  14.1 us (5%)
  starting transfers between devices  11.2 us (4%)
  local copies, waits for them, and re-layouts  11.1 us (4%)
    reduce_scatter x2, waiting for transfers between devices, sum_in_two_steps(): own = lax.psum_scatter(padded, axis, scatter_dimension=0, tiled=True)  83.2 us
    all_to_all x4, blocking collectives, copy_for_each(): lax.all_to_all(jnp.broadcast_to(array[None], (length, *array.shape)), axi...  58.6 us
    all_gather x2, waiting for transfers between devices, sum_in_two_steps(): whole = lax.all_gather(own, axis, axis=0, tiled=True)  30.2 us
    all_to_all x2, blocking collectives, sum_at_owner(): lax.all_to_all(tiles, axis, split_axis=0, concat_axis=0, tiled=True)  29.4 us
    all_gather x2, blocking collectives, correct(): lax.all_gather(own_vectors.astype(jnp.bfloat16), 'gx', axis=0, tiled=True)  14.7 us
    another operation x6, other arithmetic, solve_subspace(): lower_factor = jnp.linalg.cholesky(gram_matrix)  13 us
    another operation x4, other arithmetic, solve_subspace(): lax.linalg.triangular_solve(lower_factor, inner_solve, left_side=True, lo...  11.1 us
    all_to_all x2, starting transfers between devices, copy_for_each(): lax.all_to_all(jnp.broadcast_to(array[None], (length, *array.shape)), axi...  11.1 us
  transfers between devices with their start and end apart: 6, of which 4 were waited for; matrix products, arithmetic and copies ran while one was open for 2% of the time, Pallas kernels for 0%

commit v1 on v0

--- a/solution.py
+++ b/solution.py
@@ -41,7 +41,9 @@
     lines = array.reshape(-1, *array.shape[1:][-1:])
     padded = padded_to(lines, lax.axis_size(axis))
     own = lax.psum_scatter(padded, axis, scatter_dimension=0, tiled=True)
-    whole = lax.all_gather(own, axis, axis=0, tiled=True)
+    whole = jnp.concatenate(
+        lax.all_to_all(jnp.stack([own] * lax.axis_size(axis)), axis, 0, 0), axis=0
+    )
     return whole[: len(lines)].reshape(array.shape)
 
 

time: 310 us -> 338 us (1.090)
  waiting for transfers between devices: 113 us -> 126 us
  starting transfers between devices: 11.2 us -> 21.5 us
  local copies, waits for them, and re-layouts: 11.1 us -> 15.6 us
    all_to_all x0 -> x2, waiting for transfers between devices: none -> 80.5 us  [sum_in_two_steps(): lax.all_to_all(jnp.stack([own] * lax.axis_size(axis)), axis, 0, 0)]
    reduce_scatter x2, waiting for transfers between devices: 83.2 us -> 45.6 us  [sum_in_two_steps(): own = lax.psum_scatter(padded, axis, scatter_dimension=0, tiled=True)]
    all_gather x2 -> x0, waiting for transfers between devices: 30.2 us -> none  [sum_in_two_steps(): whole = lax.all_gather(own, axis, axis=0, tiled=True)]
    all_to_all x0 -> x2, starting transfers between devices: none -> 10.6 us  [sum_in_two_steps(): lax.all_to_all(jnp.stack([own] * lax.axis_size(axis)), axis, 0, 0)]
    another operation x0 -> x2, local copies, waits for them, and re-layouts: none -> 4.44 us  [sum_in_two_steps(): jnp.stack([own] * lax.axis_size(axis))]
where the time goes in v1:
time: 338 us; the launch traced here: 337 us
  waiting for transfers between devices  126 us (37%)
  blocking collectives  102 us (30%)
  matrix products  29.2 us (9%)
  other arithmetic  27.6 us (8%)
  starting transfers between devices  21.5 us (6%)
  local copies, waits for them, and re-layouts  15.6 us (5%)
  between operations  14.4 us (4%)
    all_to_all x2, waiting for transfers between devices, sum_in_two_steps(): lax.all_to_all(jnp.stack([own] * lax.axis_size(axis)), axis, 0, 0)  80.5 us
    all_to_all x4, blocking collectives, copy_for_each(): lax.all_to_all(jnp.broadcast_to(array[None], (length, *array.shape)), axi...  60.1 us
    reduce_scatter x2, waiting for transfers between devices, sum_in_two_steps(): own = lax.psum_scatter(padded, axis, scatter_dimension=0, tiled=True)  45.6 us
    all_to_all x2, blocking collectives, sum_at_owner(): lax.all_to_all(tiles, axis, split_axis=0, concat_axis=0, tiled=True)  28 us
    all_gather x2, blocking collectives, correct(): lax.all_gather(own_vectors.astype(jnp.bfloat16), 'gx', axis=0, tiled=True)  14.1 us
    another operation x6, other arithmetic, solve_subspace(): lower_factor = jnp.linalg.cholesky(gram_matrix)  13 us
    another operation x4, other arithmetic, solve_subspace(): lax.linalg.triangular_solve(lower_factor, inner_solve, left_side=True, lo...  11.1 us
    all_to_all x2, starting transfers between devices, copy_for_each(): lax.all_to_all(jnp.broadcast_to(array[None], (length, *array.shape)), axi...  10.8 us
  transfers between devices with their start and end apart: 6, of which 4 were waited for; matrix products, arithmetic and copies ran while one was open for 2% of the time, Pallas kernels for 0%

profile of v1, /device:TPU:2, one launch (start us, length us, event | category | flops | bytes accessed | tf_op | source)
XLA Modules:
  0.0 336.6 jit_solution(1750152803566594411)
XLA Ops:
  8.5 4.2 %fusion.17 = bf16[32,8,8,384]{3,1,2,0:T(8,128)(2,1)S(1)} fusion(bf16[384,8,512]{2,1,0:T(8,128)(2,1)} %param.8, bf16[32,8,512,1]{2,0,1,3:T(8,128)(2,1)S(1)} %bitcast.126), kind=kOutput, calls=%fused_computation.11 | convolution fusion | flops 806092800 | bytes 4980736 | tf_op jit(solution)/shard_map/prn,kln->klrp/dot_general | solution.py:108
  15.6 1.8 fusion.34
  17.5 20.0 %all_to_all.52 = bf16[8,32,384]{2,1,0:T(8,128)(2,1)} all-to-all(bf16[8,32,384]{2,1,0:T(8,128)(2,1)S(1)} %broadcast_in_dim.12), channel_id=1, replica_groups=mesh['gx'=2,'gy'=16,'gz'=8] {'gz'}, dimensions={0} | all-to-all | bytes 393216 | tf_op jit(solution)/shard_map/all_to_all | solution.py:11
  37.4 21.7 %reduce-scatter.3.cloned.1.call-done = bf16[256,384]{1,0:T(8,128)(2,1)} async-done(((bf16[2048,384]{1,0:T(8,128)(2,1)}), bf16[256,384]{1,0:T(8,128)(2,1)}) %reduce-scatter.3.cloned.1.call-update) | async-done | bytes 196624 | tf_op jit(solution)/shard_map/reduce_scatter | solution.py:43
  59.1 2.2 stack.4
  61.3 6.1 %all-to-all-start.1 = ((bf16[8,256,384]{2,1,0:T(8,128)(2,1)}), bf16[8,256,384]{2,1,0:T(8,128)(2,1)}, u32[]{:S(2)}, u32[]{:S(2)}) async-start(bf16[8,256,384]{2,1,0:T(8,128)(2,1)} %stack.4), calls=%async_computation.2 | async-start | bytes 3145728 | tf_op jit(solution)/shard_map/all_to_all | solution.py:45
  68.4 40.0 %all-to-all-done.1 = bf16[8,256,384]{2,1,0:T(8,128)(2,1)} async-done(((bf16[8,256,384]{2,1,0:T(8,128)(2,1)}), bf16[8,256,384]{2,1,0:T(8,128)(2,1)}, u32[]{:S(2)}, u32[]{:S(2)}) %all-to-all-start.1) | async-done | bytes 1572896 | tf_op jit(solution)/shard_map/all_to_all | solution.py:45
  108.3 3.3 fusion.20
  111.7 2.1 fusion.32
  113.9 13.8 %all_to_all.53 = bf16[16,16,512]{2,1,0:T(8,128)(2,1)} all-to-all(bf16[16,16,512]{2,1,0:T(8,128)(2,1)S(1)} %bitcast.123), channel_id=1, replica_groups=mesh['gx'=2,'gy'=16,'gz'=8] {'gy'}, dimensions={0} | all-to-all | bytes 524288 | tf_op jit(solution)/shard_map/all_to_all | solution.py:68
  129.5 5.7 %all-to-all-start.3 = ((bf16[16,16,512]{2,1,0:T(8,128)(2,1)}), bf16[16,16,512]{2,1,0:T(8,128)(2,1)}, u32[]{:S(2)}, u32[]{:S(2)}) async-start(bf16[16,16,512]{2,1,0:T(8,128)(2,1)} %broadcast_in_dim.13), calls=%async_computation.4 | async-start | bytes 524288 | tf_op jit(solution)/shard_map/all_to_all | solution.py:11
  135.2 7.0 %all_gather.6 = bf16[64,8,512]{2,0,1:T(8,128)(2,1)S(1)} all-gather(bf16[32,8,512]{2,0,1:T(8,128)(2,1)S(1)} %copy.159), channel_id=1, replica_groups=mesh['gx'=2,'gy'=16,'gz'=8] {'gx'}, dimensions={0}, use_global_device_ids=true | all-gather | bytes 786432 | tf_op jit(solution)/shard_map/all_gather | solution.py:89
  145.2 2.2 convolution_bitcast_fusion.6
  147.8 13.3 %all_to_all.54 = f32[8,1,6144]{2,1,0:T(1,128)S(1)} all-to-all(f32[8,1,6144]{2,1,0:T(1,128)S(1)} %broadcast_in_dim.15), channel_id=1, replica_groups=mesh['gx'=2,'gy'=16,'gz'=8] {'gz'}, dimensions={0} | all-to-all | bytes 393216 | tf_op jit(solution)/shard_map/all_to_all | solution.py:11
  161.4 5.8 %cholesky.44 = f32[64,64]{1,0:T(8,128)S(1)} custom-call(f32[64,64]{1,0:T(8,128)S(1)} %fusion.58), custom_call_target="Cholesky" | custom-call | tf_op jit(solution)/shard_map/jit(cholesky)/cholesky | solution.py:80
  168.6 4.9 %custom-call.11 = f32[1,64,64]{1,2,0:T(8,128)S(1)} custom-call(f32[1,64,64]{2,1,0:T(8,128)S(1)} %fusion.48), custom_call_target="InvertDiagBlocksLowerTriangular" | custom-call | tf_op jit(solution)/shard_map/triangular_solve/custom-call.2 | solution.py:82
  174.0 3.0 fusion.62
  177.0 2.5 fusion.14
  181.0 1.8 fusion.35
  182.8 13.1 %all_to_all.55 = bf16[8,32,384]{2,1,0:T(8,128)(2,1)S(1)} all-to-all(bf16[8,32,384]{2,1,0:T(8,128)(2,1)S(1)} %broadcast_in_dim.16), channel_id=1, replica_groups=mesh['gx'=2,'gy'=16,'gz'=8] {'gz'}, dimensions={0} | all-to-all | bytes 393216 | tf_op jit(solution)/shard_map/all_to_all | solution.py:11
  195.9 23.9 %reduce-scatter.5.cloned.1.call-done = bf16[256,384]{1,0:T(8,128)(2,1)} async-done(((bf16[2048,384]{1,0:T(8,128)(2,1)}), bf16[256,384]{1,0:T(8,128)(2,1)}) %reduce-scatter.5.cloned.1.call-update) | async-done | bytes 196624 | tf_op jit(solution)/shard_map/reduce_scatter | solution.py:43
  219.8 2.2 stack.5
  222.0 4.5 %all-to-all-start.6 = ((bf16[8,256,384]{2,1,0:T(8,128)(2,1)}), bf16[8,256,384]{2,1,0:T(8,128)(2,1)}, u32[]{:S(2)}, u32[]{:S(2)}) async-start(bf16[8,256,384]{2,1,0:T(8,128)(2,1)} %stack.5), calls=%async_computation.8 | async-start | bytes 3145728 | tf_op jit(solution)/shard_map/all_to_all | solution.py:45
  226.6 40.6 %all-to-all-done.6 = bf16[8,256,384]{2,1,0:T(8,128)(2,1)} async-done(((bf16[8,256,384]{2,1,0:T(8,128)(2,1)}), bf16[8,256,384]{2,1,0:T(8,128)(2,1)}, u32[]{:S(2)}, u32[]{:S(2)}) %all-to-all-start.6) | async-done | bytes 1572896 | tf_op jit(solution)/shard_map/all_to_all | solution.py:45
  267.1 3.3 fusion.23
  270.5 2.1 fusion.33
  272.7 14.2 %all_to_all.56 = bf16[16,16,512]{2,1,0:T(8,128)(2,1)S(1)} all-to-all(bf16[16,16,512]{2,1,0:T(8,128)(2,1)S(1)} %bitcast.124), channel_id=1, replica_groups=mesh['gx'=2,'gy'=16,'gz'=8] {'gy'}, dimensions={0} | all-to-all | bytes 524288 | tf_op jit(solution)/shard_map/all_to_all | solution.py:68
  287.7 5.1 %all-to-all-start.8 = ((bf16[16,16,512]{2,1,0:T(8,128)(2,1)}), bf16[16,16,512]{2,1,0:T(8,128)(2,1)S(1)}, u32[]{:S(2)}, u32[]{:S(2)}) async-start(bf16[16,16,512]{2,1,0:T(8,128)(2,1)} %broadcast_in_dim.17), calls=%async_computation.10 | async-start | bytes 524288 | tf_op jit(solution)/shard_map/all_to_all | solution.py:11
  292.8 7.0 %all_gather.7 = bf16[64,8,512]{2,0,1:T(8,128)(2,1)S(1)} all-gather(bf16[32,8,512]{2,0,1:T(8,128)(2,1)S(1)} %copy-done.5), channel_id=1, replica_groups=mesh['gx'=2,'gy'=16,'gz'=8] {'gx'}, dimensions={0}, use_global_device_ids=true | all-gather | bytes 786432 | tf_op jit(solution)/shard_map/all_gather | solution.py:89
  301.4 13.7 %all_to_all.57 = f32[8,1,6144]{2,1,0:T(1,128)S(1)} all-to-all(f32[8,1,6144]{2,1,0:T(1,128)S(1)} %broadcast_in_dim.18), channel_id=1, replica_groups=mesh['gx'=2,'gy'=16,'gz'=8] {'gz'}, dimensions={0} | all-to-all | bytes 393216 | tf_op jit(solution)/shard_map/all_to_all | solution.py:11
  315.4 5.8 %cholesky.55 = f32[64,64]{1,0:T(8,128)S(1)} custom-call(f32[64,64]{1,0:T(8,128)S(1)} %fusion.54), custom_call_target="Cholesky" | custom-call | tf_op jit(solution)/shard_map/jit(cholesky)/cholesky | solution.py:80
  322.6 4.9 %custom-call.13 = f32[1,64,64]{1,2,0:T(8,128)S(1)} custom-call(f32[1,64,64]{2,1,0:T(8,128)S(1)} %fusion.49), custom_call_target="InvertDiagBlocksLowerTriangular" | custom-call | tf_op jit(solution)/shard_map/triangular_solve/custom-call.2 | solution.py:82
  (76 shorter events, 20.2 us)
Async XLA Ops:
  7.2 52.0 %reduce-scatter.3.cloned.1.call-start = ((), (), s32[]{:S(2)}) async-start(), calls=%async_computation.12 | async-start | bytes 1769472 | tf_op jit(solution)/shard_map/reduce_scatter | solution.py:43
  12.8 2.9 copy-start
  61.3 47.0 %all-to-all-start.1 = ((bf16[8,256,384]{2,1,0:T(8,128)(2,1)}), bf16[8,256,384]{2,1,0:T(8,128)(2,1)}, u32[]{:S(2)}, u32[]{:S(2)}) async-start(bf16[8,256,384]{2,1,0:T(8,128)(2,1)} %stack.4), calls=%async_computation.2 | async-start | bytes 3145728 | tf_op jit(solution)/shard_map/all_to_all | solution.py:45
  113.8 31.5 %copy-start.6 = (f32[8,512]{1,0:T(8,128)S(1)}, f32[8,512]{1,0:T(8,128)}, u32[]{:S(2)}) copy-start(f32[8,512]{1,0:T(8,128)} %param.10) | copy-start | bytes 49156
  129.5 13.9 %all-to-all-start.3 = ((bf16[16,16,512]{2,1,0:T(8,128)(2,1)}), bf16[16,16,512]{2,1,0:T(8,128)(2,1)}, u32[]{:S(2)}, u32[]{:S(2)}) async-start(bf16[16,16,512]{2,1,0:T(8,128)(2,1)} %broadcast_in_dim.13), calls=%async_computation.4 | async-start | bytes 524288 | tf_op jit(solution)/shard_map/all_to_all | solution.py:11
  135.2 84.6 %reduce-scatter.5.cloned.1.call-start = ((), (), s32[]{:S(2)}) async-start(), calls=%async_computation.13 | async-start | bytes 1769472 | tf_op jit(solution)/shard_map/reduce_scatter | solution.py:43
  142.3 0.8 copy-start.1
  144.4 0.8 copy-start.2
  177.0 3.9 %copy-start.4 = (bf16[32,8,512]{2,0,1:T(8,128)(2,1)}, bf16[32,8,512]{2,0,1:T(8,128)(2,1)S(1)}, u32[]{:S(2)}) copy-start(bf16[32,8,512]{2,0,1:T(8,128)(2,1)S(1)} %get-tuple-element.13) | copy-start | bytes 786436
  222.0 45.1 %all-to-all-start.6 = ((bf16[8,256,384]{2,1,0:T(8,128)(2,1)}), bf16[8,256,384]{2,1,0:T(8,128)(2,1)}, u32[]{:S(2)}, u32[]{:S(2)}) async-start(bf16[8,256,384]{2,1,0:T(8,128)(2,1)} %stack.5), calls=%async_computation.8 | async-start | bytes 3145728 | tf_op jit(solution)/shard_map/all_to_all | solution.py:45
  270.4 22.4 %copy-start.5 = (bf16[32,8,512]{2,0,1:T(8,128)(2,1)S(1)}, bf16[32,8,512]{2,0,1:T(8,128)(2,1)}, u32[]{:S(2)}) copy-start(bf16[32,8,512]{2,0,1:T(8,128)(2,1)} %copy-done.4) | copy-start | bytes 786436
  272.6 27.7 %copy-start.3 = (f32[32,8,512]{2,0,1:T(8,128)S(1)}, f32[32,8,512]{2,0,1:T(8,128)}, u32[]{:S(2)}) copy-start(f32[32,8,512]{2,0,1:T(8,128)} %get-tuple-element.14) | copy-start | bytes 1572868
  287.7 12.5 %all-to-all-start.8 = ((bf16[16,16,512]{2,1,0:T(8,128)(2,1)}), bf16[16,16,512]{2,1,0:T(8,128)(2,1)S(1)}, u32[]{:S(2)}, u32[]{:S(2)}) async-start(bf16[16,16,512]{2,1,0:T(8,128)(2,1)} %broadcast_in_dim.17), calls=%async_computation.10 | async-start | bytes 524288 | tf_op jit(solution)/shard_map/all_to_all | solution.py:11
  328.0 1.7 copy-start.7
Sparse Core Ops, SparseCore 0:
  14.4 44.6 reduce-scatter.2
  181.1 38.6 reduce-scatter.4
